TPU v7x, 32 devices: a whole 2x2x4 slice. The times are simulated.
32 devices in a mesh: row: 4 (over x, core), col: 8 (over z, y).
Axes of the slice: x: 2, y: 2, z: 4, core: 2. Of those that a mesh axis runs over, the one named last changes fastest.
Arguments:
- matrix: float32 [2048, 2048], P('row', 'col'), as said below
- start_vectors: float32 [2048, 512], P(('col', 'row')), may hold values from -6 to 6
- interval: float32 [2], replicated, as said below
Outputs:
- ortho_basis: float32 [2048, 512], P(('col', 'row'))
- projected: float32 [512, 512], replicated
- residual: float32 [2048, 512], P(('col', 'row'))
Inputs may be any that keep to these rules, and one draw needn't show every extreme that they name: matrix is exactly symmetric (entry (r, c) equals entry (c, r)); its eigenvalues lie within about -1.45 to 1.45. interval[0] lies in [-1.2, -0.7] and interval[1] in [1.45, 1.9].
All inputs are finite; a program needn't handle non-finite values.
Results may differ from a plain program's by a relative error of at most 0.0003.
Values sent between devices are 32-bit elements.
A program may use at most 128 MiB of HBM per device.

v0:
```python
import jax
import jax.numpy as jnp
from jax import lax
from jax.sharding import PartitionSpec as P

FILTER_DEG = 3
OUTER = 2


def scattered(contribution, width, axis):
    whole = contribution(jnp.int32(0), width * lax.axis_size(axis))
    return lax.psum_scatter(whole, axis, scatter_dimension=0, tiled=True)


def spread(array, axis, root):
    mine = lax.axis_index(axis) == root
    return lax.psum(jnp.where(mine, array, jnp.zeros_like(array)), axis)


def product(left, right):
    return jnp.dot(left, right, precision=lax.Precision.HIGHEST, preferred_element_type=jnp.float32)


def tri_solve(factor, values):
    return jax.scipy.linalg.solve_triangular(factor, values, lower=True)


def on_device(matrix, start_vectors, interval):
    block_rows, block_cols = matrix.shape
    slab_rows = start_vectors.shape[0]
    total_rows = slab_rows * lax.axis_size("row") * lax.axis_size("col")
    row_index = lax.axis_index("row")
    col_index = lax.axis_index("col")
    center = 0.5 * (interval[0] + interval[1])
    half_width = 0.5 * (interval[1] - interval[0])
    global_rows = row_index * block_rows + lax.iota(jnp.int32, block_rows)
    global_cols = col_index * block_cols + lax.iota(jnp.int32, block_cols)
    diagonal = global_rows[:, None] == global_cols[None, :]
    shifted = jnp.where(diagonal, matrix - center, matrix) / half_width

    def forward(col_full):

        def term(first_row, row_count):
            strip = lax.dynamic_slice_in_dim(shifted, first_row, row_count, 0)
            return product(strip, col_full)

        return scattered(term, slab_rows, "col")

    def gather_rows(slab_part):
        return lax.all_gather(slab_part, "col", axis=0, tiled=True)

    def to_columns(row_full):
        root_row = col_index * block_cols // block_rows
        offset = col_index * block_cols - root_row * block_rows
        column_part = lax.dynamic_slice_in_dim(row_full, offset, block_cols, 0)
        return spread(column_part, "row", root_row)

    def backward(row_full):
        partial_value = lax.dot_general(
            shifted,
            row_full,
            (((0,), (0,)), ((), ())),
            precision=lax.Precision.HIGHEST,
            preferred_element_type=jnp.float32,
        )
        return lax.psum(partial_value, "row")

    current_start = lax.all_gather(start_vectors, "row", axis=0, tiled=True)
    for sweep_index in range(OUTER):
        even_cols = current_start
        odd_slab = forward(current_start)
        odd_rows = gather_rows(odd_slab)
        for degree in range(2, FILTER_DEG + 1):
            if degree % 2 == 0:
                even_cols = 2.0 * backward(odd_rows) - even_cols
            else:
                odd_slab = 2.0 * forward(even_cols) - odd_slab
                odd_rows = gather_rows(odd_slab)
        final_cols = to_columns(odd_rows)
        mapped_cols = backward(odd_rows)
        final_slab = lax.dynamic_slice_in_dim(final_cols, row_index * slab_rows, slab_rows, 0)
        mapped_slab = lax.dynamic_slice_in_dim(mapped_cols, row_index * slab_rows, slab_rows, 0)
        gram_part = product(final_slab.T, final_slab)
        cross_part = product(final_slab.T, mapped_slab)
        gram_total = lax.psum(gram_part, ("row", "col"))
        cross_total = lax.psum(cross_part, ("row", "col"))
        gram_matrix = gram_total / total_rows
        cross_terms = cross_total / total_rows
        factor = jnp.linalg.cholesky(gram_matrix)
        basis_cols = tri_solve(factor, final_cols.T).T
        partial_proj = tri_solve(factor, cross_terms)
        projected = tri_solve(factor, partial_proj.T).T
        current_start = basis_cols
    basis_slab = lax.dynamic_slice_in_dim(current_start, row_index * slab_rows, slab_rows, 0)
    residual = tri_solve(factor, mapped_slab.T).T - product(basis_slab, projected)
    return (basis_slab, projected, residual)


def solution(mesh):
    return jax.shard_map(
        on_device,
        mesh=mesh,
        in_specs=(P("row", "col"), P(("col", "row"), None), P()),
        out_specs=(P(("col", "row"), None), P(), P(("col", "row"), None)),
        check_vma=False,
    )
```

profile of v0, /device:TPU:0, one launch (start us, length us, event | category | flops | bytes accessed | tf_op | source)
XLA Modules:
  0.0 1179.7 jit_solution(1612085924572650123)
XLA Ops:
  22.0 65.1 %reduce-scatter.5.cloned.1.call-done = f32[64,512]{1,0:T(8,128)} async-done(((f32[512,512]{1,0:T(8,128)}), f32[64,512]{1,0:T(8,128)}) %reduce-scatter.5.cloned.1.call-update) | async-done | bytes 131088 | tf_op jit(solution)/shard_map/reduce_scatter | solution.py:12
  87.2 41.3 %all-gather.5.cloned.1.call-done = f32[512,512]{1,0:T(8,128)} async-done(((f32[64,512]{1,0:T(8,128)}), f32[512,512]{1,0:T(8,128)}) %all-gather.5.cloned.1.call-update) | async-done | bytes 1048592 | tf_op jit(solution)/shard_map/all_gather | solution.py:50
  132.7 32.0 %all-reduce.10.cloned.1.call-done = f32[256,512]{0,1:T(8,128)} async-done(((f32[256,512]{0,1:T(8,128)}), f32[256,512]{0,1:T(8,128)}) %all-reduce.10.cloned.1.call-update) | async-done | bytes 524304 | tf_op jit(solution)/shard_map/psum | solution.py:66
  167.9 65.6 %reduce-scatter.7.cloned.1.call-done = f32[64,512]{1,0:T(8,128)} async-done(((f32[512,512]{1,0:T(8,128)}), f32[64,512]{1,0:T(8,128)}) %reduce-scatter.7.cloned.1.call-update) | async-done | bytes 131088 | tf_op jit(solution)/shard_map/reduce_scatter | solution.py:12
  235.3 40.1 %all-gather.7.cloned.1.call-done = f32[512,512]{1,0:T(8,128)} async-done(((f32[64,512]{1,0:T(8,128)}), f32[512,512]{1,0:T(8,128)}) %all-gather.7.cloned.1.call-update) | async-done | bytes 1048592 | tf_op jit(solution)/shard_map/all_gather | solution.py:50
  277.3 33.0 %all-reduce.12.cloned.1.call-done = f32[256,512]{1,0:T(8,128)} async-done(((f32[256,512]{1,0:T(8,128)}), f32[256,512]{1,0:T(8,128)}) %all-reduce.12.cloned.1.call-update) | async-done | bytes 524304 | tf_op jit(solution)/shard_map/psum | solution.py:17
  313.5 133.4 %all-reduce.14.cloned.1.call-done = f32[512,512]{0,1:T(8,128)} async-done(((f32[512,512]{0,1:T(8,128)}), f32[512,512]{0,1:T(8,128)}) %all-reduce.14.cloned.1.call-update) | async-done | bytes 1048592 | tf_op jit(solution)/shard_map/psum | solution.py:85
  449.7 11.7 cholesky.286
  472.1 11.7 cholesky.305
  494.5 11.7 cholesky.326
  517.4 11.7 cholesky.343
  542.1 39.3 %custom-call.39 = f32[4,128,128]{1,2,0:T(8,128)S(1)} custom-call(f32[4,128,128]{2,1,0:T(8,128)S(1)} %get-tuple-element.42), custom_call_target="InvertDiagBlocksLowerTriangular" | custom-call | tf_op jit(solution)/shard_map/jit(_solve_triangular)/triangular_solve | solution.py:25
  586.6 63.4 %reduce-scatter.9.cloned.1.call-done = f32[64,512]{1,0:T(8,128)} async-done(((f32[512,512]{1,0:T(8,128)}), f32[64,512]{1,0:T(8,128)}) %reduce-scatter.9.cloned.1.call-update) | async-done | bytes 131088 | tf_op jit(solution)/shard_map/reduce_scatter | solution.py:12
  650.1 41.3 %all-gather.9.cloned.1.call-done = f32[512,512]{1,0:T(8,128)} async-done(((f32[64,512]{1,0:T(8,128)}), f32[512,512]{1,0:T(8,128)}) %all-gather.9.cloned.1.call-update) | async-done | bytes 1048592 | tf_op jit(solution)/shard_map/all_gather | solution.py:50
  695.4 32.2 %all-reduce.16.cloned.1.call-done = f32[256,512]{0,1:T(8,128)} async-done(((f32[256,512]{0,1:T(8,128)}), f32[256,512]{0,1:T(8,128)}) %all-reduce.16.cloned.1.call-update) | async-done | bytes 524304 | tf_op jit(solution)/shard_map/psum | solution.py:66
  730.8 65.8 %reduce-scatter.11.cloned.1.call-done = f32[64,512]{1,0:T(8,128)} async-done(((f32[512,512]{1,0:T(8,128)}), f32[64,512]{1,0:T(8,128)}) %reduce-scatter.11.cloned.1.call-update) | async-done | bytes 131088 | tf_op jit(solution)/shard_map/reduce_scatter | solution.py:12
  798.2 40.2 %all-gather.11.cloned.1.call-done = f32[512,512]{1,0:T(8,128)} async-done(((f32[64,512]{1,0:T(8,128)}), f32[512,512]{1,0:T(8,128)}) %all-gather.11.cloned.1.call-update) | async-done | bytes 1048592 | tf_op jit(solution)/shard_map/all_gather | solution.py:50
  842.8 35.0 %all-reduce.20.cloned.1.call-done = (f32[256,512]{1,0:T(8,128)}, f32[256,512]{1,0:T(8,128)}) async-done(((f32[256,512]{1,0:T(8,128)}, f32[256,512]{1,0:T(8,128)}), (f32[256,512]{1,0:T(8,128)}, f32[256,512]{1,0:T(8,128)})) %all-reduce.20.cloned.1.call-update) | async-done | bytes 1048592 | tf_op jit(solution)/shard_map/psum | solution.py:17
  883.7 135.3 %all-reduce.18.cloned.1.call-done = (f32[512,512]{0,1:T(8,128)}, f32[512,512]{0,1:T(8,128)}) async-done(((f32[512,512]{0,1:T(8,128)}, f32[512,512]{0,1:T(8,128)}), (f32[512,512]{0,1:T(8,128)}, f32[512,512]{0,1:T(8,128)})) %all-reduce.18.cloned.1.call-update) | async-done | bytes 2097168 | tf_op jit(solution)/shard_map/psum | solution.py:85
  1022.1 11.7 cholesky.358
  1045.1 12.1 %cholesky.377 = f32[128,128]{1,0:T(8,128)S(1)} custom-call(f32[128,128]{1,0:T(8,128)S(1)} %cholesky.443), custom_call_target="Cholesky" | custom-call | tf_op jit(solution)/shard_map/jit(cholesky)/cholesky | solution.py:89
  1068.4 11.7 cholesky.398
  1091.2 11.7 cholesky.415
  1114.8 39.5 %custom-call.43 = f32[4,128,128]{1,2,0:T(8,128)S(1)} custom-call(f32[4,128,128]{2,1,0:T(8,128)S(1)} %get-tuple-element.43), custom_call_target="InvertDiagBlocksLowerTriangular" | custom-call | tf_op jit(solution)/shard_map/jit(_solve_triangular)/triangular_solve | solution.py:25
  (193 shorter events, 177.4 us)
Async XLA Ops:
  7.2 12.7 %copy-start.10 = (f32[512,256]{1,0:T(8,128)S(1)}, f32[512,256]{1,0:T(8,128)}, u32[]{:S(2)}) copy-start(f32[512,256]{1,0:T(8,128)} %param.8) | copy-start | bytes 1572868
  7.2 80.0 %reduce-scatter.5.cloned.1.call-start = ((), (), s32[]{:S(2)}) async-start(), calls=%async_computation.4 | async-start | bytes 1179648 | tf_op jit(solution)/shard_map/reduce_scatter | solution.py:12
  22.0 106.6 %all-gather.5.cloned.1.call-start = ((), (), s32[]{:S(2)}) async-start(), calls=%async_computation.5 | async-start | bytes 1179648 | tf_op jit(solution)/shard_map/all_gather | solution.py:50
  87.2 77.6 %all-reduce.10.cloned.1.call-start = ((), (), s32[]{:S(2)}) async-start(), calls=%async_computation.6 | async-start | bytes 1048576 | tf_op jit(solution)/shard_map/psum | solution.py:66
  132.5 101.1 %reduce-scatter.7.cloned.1.call-start = ((), (), s32[]{:S(2)}) async-start(), calls=%async_computation.7 | async-start | bytes 1179648 | tf_op jit(solution)/shard_map/reduce_scatter | solution.py:12
  167.9 65.7 %copy-start.6 = (f32[64,512]{1,0:T(8,128)S(1)}, f32[64,512]{1,0:T(8,128)}, u32[]{:S(2)}) copy-start(f32[64,512]{1,0:T(8,128)} %reduce-scatter.5.cloned.1.call-done) | copy-start | bytes 393220
  167.9 107.5 %all-gather.7.cloned.1.call-start = ((), (), s32[]{:S(2)}) async-start(), calls=%async_computation.8 | async-start | bytes 1179648 | tf_op jit(solution)/shard_map/all_gather | solution.py:50
  235.2 75.1 %all-reduce.12.cloned.1.call-start = ((), (), s32[]{:S(2)}) async-start(), calls=%async_computation.9 | async-start | bytes 1048576 | tf_op jit(solution)/shard_map/psum | solution.py:17
  277.3 169.7 %all-reduce.14.cloned.1.call-start = ((), (), s32[]{:S(2)}) async-start(), calls=%async_computation.10 | async-start | bytes 2097152 | tf_op jit(solution)/shard_map/psum | solution.py:85
  313.3 336.7 %reduce-scatter.9.cloned.1.call-start = ((), (), s32[]{:S(2)}) async-start(), calls=%async_computation.11 | async-start | bytes 1179648 | tf_op jit(solution)/shard_map/reduce_scatter | solution.py:12
  448.3 1.2 copy-start.1
  533.4 48.0 %copy-start.4 = (f32[256,512]{1,0:T(8,128)S(1)}, f32[256,512]{1,0:T(8,128)}, u32[]{:S(2)}) copy-start(f32[256,512]{1,0:T(8,128)} %all-reduce.12.cloned.1.call-done) | copy-start | bytes 1572868
  586.6 104.8 %all-gather.9.cloned.1.call-start = ((), (), s32[]{:S(2)}) async-start(), calls=%async_computation.12 | async-start | bytes 1179648 | tf_op jit(solution)/shard_map/all_gather | solution.py:50
  650.0 77.6 %all-reduce.16.cloned.1.call-start = ((), (), s32[]{:S(2)}) async-start(), calls=%async_computation.13 | async-start | bytes 1048576 | tf_op jit(solution)/shard_map/psum | solution.py:66
  695.3 101.2 %reduce-scatter.11.cloned.1.call-start = ((), (), s32[]{:S(2)}) async-start(), calls=%async_computation.14 | async-start | bytes 1179648 | tf_op jit(solution)/shard_map/reduce_scatter | solution.py:12
  730.7 65.8 %copy-start.5 = (f32[64,512]{1,0:T(8,128)S(1)}, f32[64,512]{1,0:T(8,128)}, u32[]{:S(2)}) copy-start(f32[64,512]{1,0:T(8,128)} %reduce-scatter.9.cloned.1.call-done) | copy-start | bytes 393220
  730.7 107.6 %all-gather.11.cloned.1.call-start = ((), (), s32[]{:S(2)}) async-start(), calls=%async_computation.15 | async-start | bytes 1179648 | tf_op jit(solution)/shard_map/all_gather | solution.py:50
  798.2 79.6 %all-reduce.20.cloned.1.call-start = ((), (), s32[]{:S(2)}) async-start(), calls=%async_computation.17 | async-start | bytes 2097152 | tf_op jit(solution)/shard_map/psum | solution.py:17
  838.4 3.3 copy-start.7
  842.6 176.4 %all-reduce.18.cloned.1.call-start = ((), (), s32[]{:S(2)}) async-start(), calls=%async_computation.16 | async-start | bytes 4194304 | tf_op jit(solution)/shard_map/psum | solution.py:85
  877.8 3.0 copy-start.8
  1019.0 2.4 copy-start
  1154.7 1.3 copy-start.3
  1158.0 2.1 copy-start.2
  (2 other events, 1.8 us)
Sparse Core Ops, SparseCore 0:
  22.1 65.0 reduce-scatter.4
  89.3 39.2 all-gather.4
  132.6 32.0 all-reduce.9
  168.6 64.9 reduce-scatter.6
  236.1 39.1 all-gather.6
  278.2 32.0 all-reduce.11
  316.1 130.8 all-reduce.13
  586.7 63.2 reduce-scatter.8
  652.1 39.2 all-gather.8
  695.4 32.1 all-reduce.15
  731.6 64.9 reduce-scatter.10
  799.1 39.2 all-gather.10
  842.7 35.0 all-reduce.19
  883.8 135.1 all-reduce.17
where the time goes:
time: 1190 us; the launch traced here: 1180 us
  waiting for transfers between devices  824 us (69%)
  other arithmetic  248 us (21%)
  matrix products  53.3 us (4%)
  between operations  22.6 us (2%)
  local copies, waits for them, and re-layouts  22.2 us (2%)
    psum x2, waiting for transfers between devices, on_device(): gram_total = lax.psum(gram_part, ('row', 'col'))  269 us
    reduce_scatter x4, waiting for transfers between devices, scattered(): return lax.psum_scatter(whole, axis, scatter_dimension=0, tiled=True)  260 us
    all_gather x4, waiting for transfers between devices, gather_rows(): return lax.all_gather(slab_part, 'col', axis=0, tiled=True)  163 us
    another operation x29, other arithmetic, on_device(): factor = jnp.linalg.cholesky(gram_matrix)  158 us
    another operation x6, other arithmetic, tri_solve(): return jax.scipy.linalg.solve_triangular(factor, values, lower=True)  79.2 us
    psum x2, waiting for transfers between devices, spread(): return lax.psum(jnp.where(mine, array, jnp.zeros_like(array)), axis)  67.9 us
    psum x2, waiting for transfers between devices, backward(): return lax.psum(partial_value, 'row')  64.2 us
  transfers between devices with their start and end apart: 14, of which 14 were waited for; matrix products, arithmetic and copies ran while one was open for 0% of the time, Pallas kernels for 0%

commit v1 on v0

--- a/solution.py
+++ b/solution.py
@@ -82,7 +82,8 @@
         mapped_slab = lax.dynamic_slice_in_dim(mapped_cols, row_index * slab_rows, slab_rows, 0)
         gram_part = product(final_slab.T, final_slab)
         cross_part = product(final_slab.T, mapped_slab)
-        gram_total = lax.psum(gram_part, ("row", "col"))
+        one_axis = lax.psum(gram_part, "col")
+        gram_total = lax.psum(one_axis, "row")
         cross_total = lax.psum(cross_part, ("row", "col"))
         gram_matrix = gram_total / total_rows
         cross_terms = cross_total / total_rows

time: 1190 us -> 1280 us (1.076)
  waiting for transfers between devices: 824 us -> 921 us
    psum x2 -> x5, waiting for transfers between devices: 269 us -> 366 us  [the longest x2 157 us: on_device(): one_axis = lax.psum(gram_part, 'col')]
  transfers between devices with their start and end apart: 14 -> 17, of which waited for: 14 -> 17; matrix products, arithmetic and copies ran while one was open for 0% -> 1% of each run, Pallas kernels for 0% -> 0%
where the time goes in v1:
time: 1280 us
  waiting for transfers between devices  921 us (72%)
  other arithmetic  249 us (19%)
  matrix products  51 us (4%)
  local copies, waits for them, and re-layouts  22.6 us (2%)
  between operations  22.6 us (2%)
    reduce_scatter x4, waiting for transfers between devices, scattered(): return lax.psum_scatter(whole, axis, scatter_dimension=0, tiled=True)  261 us
    all_gather x4, waiting for transfers between devices, gather_rows(): return lax.all_gather(slab_part, 'col', axis=0, tiled=True)  163 us
    another operation x29, other arithmetic, on_device(): factor = jnp.linalg.cholesky(gram_matrix)  158 us
    psum x2, waiting for transfers between devices, on_device(): one_axis = lax.psum(gram_part, 'col')  157 us
    psum x1, waiting for transfers between devices, on_device(): cross_total = lax.psum(cross_part, ('row', 'col'))  126 us
    psum x2, waiting for transfers between devices, on_device(): gram_total = lax.psum(one_axis, 'row')  82.6 us
    another operation x6, other arithmetic, tri_solve(): return jax.scipy.linalg.solve_triangular(factor, values, lower=True)  79.2 us
    psum x2, waiting for transfers between devices, spread(): return lax.psum(jnp.where(mine, array, jnp.zeros_like(array)), axis)  65.9 us
  transfers between devices with their start and end apart: 17, of which 17 were waited for; matrix products, arithmetic and copies ran while one was open for 1% of the time, Pallas kernels for 0%

profile of v1, /device:TPU:0, one launch (start us, length us, event | category | flops | bytes accessed | tf_op | source)
XLA Modules:
  0.0 1275.9 jit_solution(11193210304757238607)
XLA Ops:
  22.0 65.2 %reduce-scatter.5.cloned.1.call-done = f32[64,512]{1,0:T(8,128)} async-done(((f32[512,512]{1,0:T(8,128)}), f32[64,512]{1,0:T(8,128)}) %reduce-scatter.5.cloned.1.call-update) | async-done | bytes 131088 | tf_op jit(solution)/shard_map/reduce_scatter | solution.py:12
  87.3 41.3 %all-gather.5.cloned.1.call-done = f32[512,512]{1,0:T(8,128)} async-done(((f32[64,512]{1,0:T(8,128)}), f32[512,512]{1,0:T(8,128)}) %all-gather.5.cloned.1.call-update) | async-done | bytes 1048592 | tf_op jit(solution)/shard_map/all_gather | solution.py:50
  132.8 32.0 %all-reduce.12.cloned.1.call-done = f32[256,512]{0,1:T(8,128)} async-done(((f32[256,512]{0,1:T(8,128)}), f32[256,512]{0,1:T(8,128)}) %all-reduce.12.cloned.1.call-update) | async-done | bytes 524304 | tf_op jit(solution)/shard_map/psum | solution.py:66
  168.0 65.6 %reduce-scatter.7.cloned.1.call-done = f32[64,512]{1,0:T(8,128)} async-done(((f32[512,512]{1,0:T(8,128)}), f32[64,512]{1,0:T(8,128)}) %reduce-scatter.7.cloned.1.call-update) | async-done | bytes 131088 | tf_op jit(solution)/shard_map/reduce_scatter | solution.py:12
  235.4 40.1 %all-gather.7.cloned.1.call-done = f32[512,512]{1,0:T(8,128)} async-done(((f32[64,512]{1,0:T(8,128)}), f32[512,512]{1,0:T(8,128)}) %all-gather.7.cloned.1.call-update) | async-done | bytes 1048592 | tf_op jit(solution)/shard_map/all_gather | solution.py:50
  277.4 33.0 %all-reduce.14.cloned.1.call-done = f32[256,512]{1,0:T(8,128)} async-done(((f32[256,512]{1,0:T(8,128)}), f32[256,512]{1,0:T(8,128)}) %all-reduce.14.cloned.1.call-update) | async-done | bytes 524304 | tf_op jit(solution)/shard_map/psum | solution.py:17
  313.4 79.5 %all-reduce.16.cloned.1.call-done = f32[512,512]{0,1:T(8,128)} async-done(((f32[512,512]{0,1:T(8,128)}), f32[512,512]{0,1:T(8,128)}) %all-reduce.16.cloned.1.call-update) | async-done | bytes 1048592 | tf_op jit(solution)/shard_map/psum | solution.py:85
  393.2 38.0 %all-reduce.18.cloned.1.call-done = f32[512,512]{0,1:T(8,128)} async-done(((f32[512,512]{0,1:T(8,128)}), f32[512,512]{0,1:T(8,128)}) %all-reduce.18.cloned.1.call-update) | async-done | bytes 1048592 | tf_op jit(solution)/shard_map/psum | solution.py:86
  434.0 11.7 cholesky.286
  456.4 11.7 cholesky.305
  478.8 11.7 cholesky.326
  501.7 11.7 cholesky.343
  526.4 39.3 %custom-call.39 = f32[4,128,128]{1,2,0:T(8,128)S(1)} custom-call(f32[4,128,128]{2,1,0:T(8,128)S(1)} %get-tuple-element.42), custom_call_target="InvertDiagBlocksLowerTriangular" | custom-call | tf_op jit(solution)/shard_map/jit(_solve_triangular)/triangular_solve | solution.py:25
  570.9 64.8 %reduce-scatter.9.cloned.1.call-done = f32[64,512]{1,0:T(8,128)} async-done(((f32[512,512]{1,0:T(8,128)}), f32[64,512]{1,0:T(8,128)}) %reduce-scatter.9.cloned.1.call-update) | async-done | bytes 131088 | tf_op jit(solution)/shard_map/reduce_scatter | solution.py:12
  635.8 41.2 %all-gather.9.cloned.1.call-done = f32[512,512]{1,0:T(8,128)} async-done(((f32[64,512]{1,0:T(8,128)}), f32[512,512]{1,0:T(8,128)}) %all-gather.9.cloned.1.call-update) | async-done | bytes 1048592 | tf_op jit(solution)/shard_map/all_gather | solution.py:50
  681.0 32.2 %all-reduce.20.cloned.1.call-done = f32[256,512]{0,1:T(8,128)} async-done(((f32[256,512]{0,1:T(8,128)}), f32[256,512]{0,1:T(8,128)}) %all-reduce.20.cloned.1.call-update) | async-done | bytes 524304 | tf_op jit(solution)/shard_map/psum | solution.py:66
  716.4 65.6 %reduce-scatter.11.cloned.1.call-done = f32[64,512]{1,0:T(8,128)} async-done(((f32[512,512]{1,0:T(8,128)}), f32[64,512]{1,0:T(8,128)}) %reduce-scatter.11.cloned.1.call-update) | async-done | bytes 131088 | tf_op jit(solution)/shard_map/reduce_scatter | solution.py:12
  783.7 40.3 %all-gather.11.cloned.1.call-done = f32[512,512]{1,0:T(8,128)} async-done(((f32[64,512]{1,0:T(8,128)}), f32[512,512]{1,0:T(8,128)}) %all-gather.11.cloned.1.call-update) | async-done | bytes 1048592 | tf_op jit(solution)/shard_map/all_gather | solution.py:50
  825.9 33.0 %all-reduce.22.cloned.1.call-done = f32[256,512]{1,0:T(8,128)} async-done(((f32[256,512]{1,0:T(8,128)}), f32[256,512]{1,0:T(8,128)}) %all-reduce.22.cloned.1.call-update) | async-done | bytes 524304 | tf_op jit(solution)/shard_map/psum | solution.py:17
  864.0 77.4 %all-reduce.24.cloned.1.call-done = f32[512,512]{0,1:T(8,128)} async-done(((f32[512,512]{0,1:T(8,128)}), f32[512,512]{0,1:T(8,128)}) %all-reduce.24.cloned.1.call-update) | async-done | bytes 1048592 | tf_op jit(solution)/shard_map/psum | solution.py:85
  941.6 44.6 %all-reduce.28.cloned.1.call-done = (f32[512,512]{0,1:T(8,128)}, f32[256,512]{1,0:T(8,128)}) async-done(((f32[512,512]{0,1:T(8,128)}, f32[256,512]{1,0:T(8,128)}), (f32[512,512]{0,1:T(8,128)}, f32[256,512]{1,0:T(8,128)})) %all-reduce.28.cloned.1.call-update) | async-done | bytes 1572880 | tf_op jit(solution)/shard_map/psum | solution.py:86
  1058.2 11.7 cholesky.415
  1081.3 39.5 %custom-call.43 = f32[4,128,128]{1,2,0:T(8,128)S(1)} custom-call(f32[4,128,128]{2,1,0:T(8,128)S(1)} %get-tuple-element.43), custom_call_target="InvertDiagBlocksLowerTriangular" | custom-call | tf_op jit(solution)/shard_map/jit(_solve_triangular)/triangular_solve | solution.py:25
  1128.5 126.4 %all-reduce.26.cloned.1.call-done = f32[512,512]{0,1:T(8,128)} async-done(((f32[512,512]{0,1:T(8,128)}), f32[512,512]{0,1:T(8,128)}) %all-reduce.26.cloned.1.call-update) | async-done | bytes 1048592 | tf_op jit(solution)/shard_map/psum | solution.py:87
  (200 shorter events, 211.9 us)
Async XLA Ops:
  7.2 12.7 copy-start.9
  7.2 80.1 %reduce-scatter.5.cloned.1.call-start = ((), (), s32[]{:S(2)}) async-start(), calls=%async_computation.4 | async-start | bytes 1179648 | tf_op jit(solution)/shard_map/reduce_scatter | solution.py:12
  22.0 106.6 %all-gather.5.cloned.1.call-start = ((), (), s32[]{:S(2)}) async-start(), calls=%async_computation.5 | async-start | bytes 1179648 | tf_op jit(solution)/shard_map/all_gather | solution.py:50
  87.3 77.6 %all-reduce.12.cloned.1.call-start = ((), (), s32[]{:S(2)}) async-start(), calls=%async_computation.6 | async-start | bytes 1048576 | tf_op jit(solution)/shard_map/psum | solution.py:66
  132.6 101.1 %reduce-scatter.7.cloned.1.call-start = ((), (), s32[]{:S(2)}) async-start(), calls=%async_computation.7 | async-start | bytes 1179648 | tf_op jit(solution)/shard_map/reduce_scatter | solution.py:12
  168.0 65.7 %copy-start.5 = (f32[64,512]{1,0:T(8,128)S(1)}, f32[64,512]{1,0:T(8,128)}, u32[]{:S(2)}) copy-start(f32[64,512]{1,0:T(8,128)} %reduce-scatter.5.cloned.1.call-done) | copy-start | bytes 393220
  168.0 107.5 %all-gather.7.cloned.1.call-start = ((), (), s32[]{:S(2)}) async-start(), calls=%async_computation.8 | async-start | bytes 1179648 | tf_op jit(solution)/shard_map/all_gather | solution.py:50
  235.3 75.1 %all-reduce.14.cloned.1.call-start = ((), (), s32[]{:S(2)}) async-start(), calls=%async_computation.9 | async-start | bytes 1048576 | tf_op jit(solution)/shard_map/psum | solution.py:17
  277.4 115.6 %all-reduce.16.cloned.1.call-start = ((), (), s32[]{:S(2)}) async-start(), calls=%async_computation.10 | async-start | bytes 2097152 | tf_op jit(solution)/shard_map/psum | solution.py:85
  313.4 117.8 %all-reduce.18.cloned.1.call-start = ((), (), s32[]{:S(2)}) async-start(), calls=%async_computation.11 | async-start | bytes 2097152 | tf_op jit(solution)/shard_map/psum | solution.py:86
  393.0 242.8 %reduce-scatter.9.cloned.1.call-start = ((), (), s32[]{:S(2)}) async-start(), calls=%async_computation.12 | async-start | bytes 1179648 | tf_op jit(solution)/shard_map/reduce_scatter | solution.py:12
  432.6 1.2 copy-start.1
  517.7 48.0 %copy-start.3 = (f32[256,512]{1,0:T(8,128)S(1)}, f32[256,512]{1,0:T(8,128)}, u32[]{:S(2)}) copy-start(f32[256,512]{1,0:T(8,128)} %all-reduce.14.cloned.1.call-done) | copy-start | bytes 1572868
  570.9 106.1 %all-gather.9.cloned.1.call-start = ((), (), s32[]{:S(2)}) async-start(), calls=%async_computation.13 | async-start | bytes 1179648 | tf_op jit(solution)/shard_map/all_gather | solution.py:50
  635.7 77.5 %all-reduce.20.cloned.1.call-start = ((), (), s32[]{:S(2)}) async-start(), calls=%async_computation.14 | async-start | bytes 1048576 | tf_op jit(solution)/shard_map/psum | solution.py:66
  681.0 101.1 %reduce-scatter.11.cloned.1.call-start = ((), (), s32[]{:S(2)}) async-start(), calls=%async_computation.15 | async-start | bytes 1179648 | tf_op jit(solution)/shard_map/reduce_scatter | solution.py:12
  716.3 65.7 %copy-start.4 = (f32[64,512]{1,0:T(8,128)S(1)}, f32[64,512]{1,0:T(8,128)}, u32[]{:S(2)}) copy-start(f32[64,512]{1,0:T(8,128)} %reduce-scatter.9.cloned.1.call-done) | copy-start | bytes 393220
  716.4 107.6 %all-gather.11.cloned.1.call-start = ((), (), s32[]{:S(2)}) async-start(), calls=%async_computation.16 | async-start | bytes 1179648 | tf_op jit(solution)/shard_map/all_gather | solution.py:50
  783.7 75.2 %all-reduce.22.cloned.1.call-start = ((), (), s32[]{:S(2)}) async-start(), calls=%async_computation.17 | async-start | bytes 1048576 | tf_op jit(solution)/shard_map/psum | solution.py:17
  825.9 36.1 %copy-start.6 = (f32[512,512]{1,0:T(8,128)S(1)}, f32[512,512]{1,0:T(8,128)}, u32[]{:S(2)}) copy-start(f32[512,512]{1,0:T(8,128)} %all-gather.11.cloned.1.call-done) | copy-start | bytes 3145732
  825.9 115.5 %all-reduce.24.cloned.1.call-start = ((), (), s32[]{:S(2)}) async-start(), calls=%async_computation.18 | async-start | bytes 2097152 | tf_op jit(solution)/shard_map/psum | solution.py:85
  861.9 124.3 %all-reduce.28.cloned.1.call-start = ((), (), s32[]{:S(2)}) async-start(), calls=%async_computation.20 | async-start | bytes 3145728 | tf_op jit(solution)/shard_map/psum | solution.py:86
  941.4 313.5 %all-reduce.26.cloned.1.call-start = ((), (), s32[]{:S(2)}) async-start(), calls=%async_computation.19 | async-start | bytes 2097152 | tf_op jit(solution)/shard_map/psum | solution.py:87
  1073.1 47.7 %copy-start.7 = (f32[256,512]{1,0:T(8,128)S(1)}, f32[256,512]{1,0:T(8,128)}, u32[]{:S(2)}) copy-start(f32[256,512]{1,0:T(8,128)} %get-tuple-element.69) | copy-start | bytes 1572868
  (4 other events, 4.2 us)
Sparse Core Ops, SparseCore 0:
  22.1 65.0 reduce-scatter.4
  89.4 39.2 all-gather.4
  132.7 32.0 all-reduce.11
  168.7 64.9 reduce-scatter.6
  236.2 39.1 all-gather.6
  278.2 32.0 all-reduce.13
  314.5 78.4 all-reduce.15
  395.3 35.8 all-reduce.17
  571.0 64.6 reduce-scatter.8
  637.7 39.2 all-gather.8
  681.1 32.0 all-reduce.19
  717.1 64.9 reduce-scatter.10
  784.8 39.1 all-gather.10
  826.8 32.1 all-reduce.21
  862.8 78.4 all-reduce.23
  943.7 42.4 all-reduce.27
  1124.1 130.7 all-reduce.25
